TPU v7x, 256 devices: a whole 4x4x8 slice. The times are simulated.
256 devices in a mesh: dp: 32 (over x, z), tensor: 8 (over y, core).
Axes of the slice: x: 4, y: 4, z: 8, core: 2. Of those that a mesh axis runs over, the one named last changes fastest.
Arguments:
- vis_rows: bfloat16 [8, 256, 2, 3200], P(None, 'dp', None, 'tensor'), may hold values from -6 to 6
- ln_gain: float32 [2, 3200], replicated, may hold values from 0.25 to 1.75
- ln_bias: float32 [2, 3200], replicated, may hold values from -3 to 3
- proj_weight: bfloat16 [3200, 2, 8192], P('dp', None, 'tensor'), may hold values from -0.078125 to 0.078125
- text_rows: bfloat16 [32, 384, 8192], P('dp', None, 'tensor'), may hold values from -8 to 8
- attn_gain: float32 [8192], replicated, may hold values from 0.25 to 1.75
- w_query: bfloat16 [8192, 4096], P('dp', 'tensor'), may hold values from -0.088388348 to 0.088388348
- key_value_weight: bfloat16 [8192, 2, 1024], P('dp', None, 'tensor'), may hold values from -0.088388348 to 0.088388348
- tile_counts: int32 [32], replicated, may hold values from 1 to 16, 256 in all
- image_offsets: int32 [32], P('dp'), may hold values from 0 to 256
Outputs:
- attn_context: bfloat16 [32, 384, 4096], P('dp', None, 'tensor')
Inputs may be any that keep to these rules, and one draw needn't show every extreme that they name: tile_counts counts all 256 tiles, and its largest entry is exactly 16.
All inputs are finite; a program needn't handle non-finite values.
Results may differ from a plain program's by a relative error of at most 0.0074.
Values may be sent and summed in bfloat16 or wider, within the bound.
No kernel may reach another device: no remote copies, remote signals or barrier semaphores. Data moves between devices by JAX's collectives and lax.ppermute only.
A program may use at most 128 MiB of HBM per device.

v0:
```python
import jax
import jax.numpy as jnp
from jax import lax
from jax.experimental import pallas as pl
from jax.experimental.pallas import tpu as pltpu
from jax.sharding import Mesh, PartitionSpec as P


HEAD = 128
NX, NZ, NY, NC = 4, 8, 4, 2
SEQ = 384
SPAN = 128
WIDTH = 8192
vision_epsilon = 1e-06
decoder_epsilon = 1e-05
rope_base = 500000.0


def shift(array, axis, by):
    size = lax.axis_size(axis)
    return lax.ppermute(array, axis, [(i, (i + by) % size) for i in range(size)])


def flip_x(array, flip):
    return lax.ppermute(array, "x", [(i, i ^ flip) for i in range(NX)])


def exchange(array, axis):
    return lax.all_to_all(array, axis, 0, 0, tiled=True)


def spread(array, axis):
    size = lax.axis_size(axis)
    return exchange(jnp.broadcast_to(array[None], (size, *array.shape)), axis)


def ring4(array, axis):
    half = array.shape[0] // 2
    below = shift(array, axis, 1)
    above = shift(array, axis, -1)
    far_low = shift(below[:half], axis, 1)
    far_high = shift(above[half:], axis, -1)
    return [(array, 0, 0), (below, -1, 0), (above, 1, 0), (far_low, 2, 0), (far_high, 2, half)]


def ring8(array, axis, half):
    pieces = [(array, 0)]
    below = above = array
    for step in (1, 2, 3):
        below = shift(below, axis, 1)
        above = shift(above, axis, -1)
        pieces += [(below, -step), (above, step)]
    far = [shift(below[:half], axis, 1), shift(above[half:], axis, -1)]
    return pieces + [(jnp.concatenate(far, axis=0), 4)]


def rope_tables():
    half = HEAD // 2
    exponents = jnp.arange(half, dtype=jnp.float32) * (2.0 / HEAD)
    frequency = rope_base ** (-exponents)
    positions = jnp.arange(SEQ, dtype=jnp.int32).astype(jnp.float32)
    angles = positions[:, None] * frequency[None, :]
    cosine, sine = jnp.cos(angles), jnp.sin(angles)
    return (
        jnp.concatenate([cosine, cosine], axis=1),
        jnp.concatenate([-sine, sine], axis=1),
    )


VMEM = pl.BlockSpec(memory_space=pltpu.VMEM)
SMEM = pl.BlockSpec(memory_space=pltpu.SMEM)
HBM = pl.BlockSpec(memory_space=pltpu.HBM)


def rotated(value, cos, sin):
    return (value * cos + pltpu.roll(value, 64, 1) * sin).astype(jnp.bfloat16)


def decoder(where, text, image, gain, weight, cosine, sine):
    arrays = [a for a, _, _, _ in text] + list(image)
    n_text, count = len(text), len(arrays)

    def kernel(where_ref, *refs):
        gain_ref, w_hbm, cos_ref, sin_ref, out_ref, a_ref, w_ref, w_sem = refs[count:]
        loads = []
        for t in range(8):
            rows = pl.ds(t * 1024, 1024)
            loads.append(pltpu.make_async_copy(w_hbm.at[rows, :], w_ref.at[rows, :], w_sem.at[t]))
            loads[-1].start()
        y, c = where_ref[0], where_ref[1]
        start, n_rows = where_ref[2], where_ref[3]
        total = None
        for n, (_, dy, first, flip) in enumerate(text):
            rows = refs[n].shape[0]
            side = lax.rem(y + (dy + NY), NY)
            t = side * NC + (c if flip == 0 else 1 - c)
            p_at = lax.broadcasted_iota(jnp.int32, (rows, SPAN), 0) + first - start
            j_at = lax.broadcasted_iota(jnp.int32, (rows, SPAN), 1)
            pick = jnp.where((p_at == j_at) & (j_at < n_rows), 1.0, 0.0).astype(jnp.bfloat16)
            rows_at = lax.broadcasted_iota(jnp.int32, (rows, 1), 0) + first - start
            is_image = (rows_at >= 0) & (rows_at < n_rows)
            placed = jnp.dot(
                pick, refs[n_text + flip][side], preferred_element_type=jnp.float32
            )
            value = jnp.where(is_image, placed, refs[n][...].astype(jnp.float32))
            a_ref[t, first : first + rows, :] = value.astype(jnp.bfloat16)
            squares = jnp.sum(value * value, axis=1, keepdims=True)
            if rows < SEQ:
                zero = jnp.zeros((SEQ - rows, 1), jnp.float32)
                squares = jnp.concatenate([squares, zero] if first == 0 else [zero, squares], axis=0)
            total = squares if total is None else total + squares
        scale = lax.rsqrt(total * (1.0 / WIDTH) + decoder_epsilon)
        acc = jnp.zeros((SEQ, 768), jnp.float32)
        for t in range(8):
            normed = (
                a_ref[t].astype(jnp.float32) * scale * gain_ref[t : t + 1, :]
            ).astype(jnp.bfloat16)
            loads[t].wait()
            acc = acc + jnp.dot(
                normed, w_ref[t * 1024 : (t + 1) * 1024, :], preferred_element_type=jnp.float32
            )
        cos, sin = cos_ref[...], sin_ref[...]
        key = rotated(acc[:, 512:640], cos, sin)
        value = acc[:, 640:].astype(jnp.bfloat16)
        at = lax.broadcasted_iota(jnp.int32, (SEQ, SEQ), 0)
        causal = at >= lax.broadcasted_iota(jnp.int32, (SEQ, SEQ), 1)
        for h in range(4):
            query = rotated(acc[:, h * HEAD : (h + 1) * HEAD], cos, sin)
            scores = lax.dot_general(
                query, key, (((1,), (1,)), ((), ())), preferred_element_type=jnp.float32
            ) * (HEAD ** (-0.5))
            scores = jnp.where(causal, scores, -1e30)
            top = jnp.max(scores, axis=1, keepdims=True)
            e = jnp.exp(scores - top)
            w = (e * (1.0 / jnp.sum(e, axis=1, keepdims=True))).astype(jnp.bfloat16)
            out_ref[:, h * HEAD : (h + 1) * HEAD] = jnp.dot(
                w, value, preferred_element_type=jnp.float32
            ).astype(jnp.bfloat16)

    return pl.pallas_call(
        kernel,
        out_shape=jax.ShapeDtypeStruct((SEQ, 512), jnp.bfloat16),
        in_specs=[SMEM] + [VMEM] * (count + 1) + [HBM] + [VMEM] * 2,
        out_specs=VMEM,
        scratch_shapes=[
            pltpu.VMEM((8, SEQ, 1024), jnp.bfloat16),
            pltpu.VMEM((WIDTH, 768), jnp.bfloat16),
            pltpu.SemaphoreType.DMA((8,)),
        ],
        compiler_params=pltpu.CompilerParams(vmem_limit_bytes=52 * 1024 * 1024),
        name="decoder",
    )(where, *arrays, gain, weight, cosine, sine)


def vision(vis_rows, ln_gain, ln_bias, proj_weight, z):
    tokens = vis_rows.shape[0] * vis_rows.shape[1]
    whole = spread(vis_rows.reshape(tokens, 2, 400), ("y", "c")).astype(jnp.float32)
    mean = jnp.mean(whole, axis=(0, 2, 3))[None, :, None, None]
    centered = whole - mean
    variance = jnp.mean(centered * centered, axis=(0, 2, 3))[None, :, None, None]
    gain = jnp.swapaxes(ln_gain.reshape(2, 8, 400), 0, 1)[:, None]
    bias = jnp.swapaxes(ln_bias.reshape(2, 8, 400), 0, 1)[:, None]
    normed = (centered * lax.rsqrt(variance + vision_epsilon) * gain + bias).astype(jnp.bfloat16)
    acts = exchange(normed.reshape(4, 2, tokens, 2, 400), "x")
    blocks = acts.reshape(4, 2, tokens, 2, 4, 100)
    blocks = jnp.transpose(blocks, (1, 4, 0, 2, 3, 5)).reshape(8, 4 * tokens, 200)
    own = jnp.swapaxes(proj_weight, 0, 1).reshape(200, 1024)
    partial = None
    for piece, dz in ring8(own, "z", 96):
        block = lax.dynamic_index_in_dim(blocks, lax.rem(z + dz + NZ, NZ), 0, keepdims=False)
        term = jnp.dot(block, piece, preferred_element_type=jnp.float32)
        partial = term if partial is None else partial + term
    partial = partial.astype(jnp.bfloat16).reshape(4, tokens, 1024)
    total = None
    for k in range(NX):
        part = lax.dynamic_index_in_dim(partial, lax.axis_index("x") ^ k, 0, keepdims=False)
        part = (part if k == 0 else flip_x(part, k)).astype(jnp.float32)
        total = part if total is None else total + part
    return total.astype(jnp.bfloat16)


def step(
    vis_rows, ln_gain, ln_bias, proj_weight, text_rows, attn_gain, w_query,
    key_value_weight, tile_counts, image_offsets,
):
    x, z = lax.axis_index("x"), lax.axis_index("z")
    y, c = lax.axis_index("y"), lax.axis_index("c")
    tile_ends = jnp.cumsum(tile_counts)
    tile_firsts = tile_ends - tile_counts
    sample_ids = jnp.arange(32, dtype=jnp.int32)

    def entry(values, index):
        return jnp.sum(jnp.where(sample_ids == index, values, 0))

    both = jnp.concatenate([w_query, key_value_weight.reshape(256, 256)], axis=1)
    both_all = lax.all_gather(both, ("x", "z"), axis=0, tiled=True)

    image = vision(vis_rows, ln_gain, ln_bias, proj_weight, z).reshape(8, 8, 1024)

    text = []
    for a, dy, row in ring4(text_rows[0], "y"):
        text.append((a, dy, row, 0))
        text.append((shift(a, "c", 1), dy, row, 1))

    place = x * NZ + z
    tiles_here = jnp.arange(8, dtype=jnp.int32) * 32 + place
    owners = jnp.sum((tile_ends[None, :] <= tiles_here[:, None]).astype(jnp.int32), axis=1)
    slots = jnp.zeros((32, 8, 1024), jnp.bfloat16)
    for r in range(8):
        slots = jnp.where((owners[r] == sample_ids)[:, None, None], image[r][None], slots)
    received = exchange(slots, ("x", "z"))
    sources = (entry(tile_firsts, place) + jnp.arange(16, dtype=jnp.int32)) % 32
    mine = received[sources].reshape(SPAN, 1024)
    own_image = spread(mine, "y")
    other_image = shift(own_image, "c", 1)

    rows = entry(tile_counts, place) * 8
    where = jnp.stack([y, c, image_offsets[0], rows]).astype(jnp.int32)
    cosine, sine = rope_tables()
    gain = attn_gain.reshape(8, 1024)
    out = decoder(where, text, (own_image, other_image), gain, both_all, cosine, sine)
    return out[None]


def solution(mesh):
    fine = Mesh(mesh.devices.reshape(NX, NZ, NY, NC), ("x", "z", "y", "c"))
    dp, tensor = ("x", "z"), ("y", "c")
    in_specs = (
        P(None, dp, None, tensor), P(), P(), P(dp, None, tensor), P(dp, None, tensor), P(),
        P(dp, tensor), P(dp, None, tensor), P(), P(dp),
    )
    return jax.shard_map(
        step, mesh=fine, in_specs=in_specs, out_specs=P(dp, None, tensor), check_vma=False
    )
```

profile of v0, /device:TPU:1, one launch (start us, length us, event | category | flops | bytes accessed | tf_op | source)
XLA Modules:
  0.0 197.4 jit_solution(14938277578854431626)
XLA Ops:
  6.5 0.9 copy.32
  7.5 1.7 pad_maximum_fusion
  9.2 1.0 copy.25
  10.2 1.1 broadcast_in_dim.131
  11.3 6.8 %all-to-all-start = ((bf16[8,64,2,400]{3,1,2,0:T(8,128)(2,1)}), bf16[8,64,2,400]{3,1,2,0:T(8,128)(2,1)S(1)}, u32[]{:S(2)}, u32[]{:S(2)}) async-start(bf16[8,64,2,400]{3,1,2,0:T(8,128)(2,1)} %broadcast_in_dim.131), calls=%async_computation | async-start | bytes 2097152 | tf_op jit(solution)/shard_map/all_to_all | solution.py:29
  18.2 5.0 %collective-permute-start.10 = (bf16[200,1024]{1,0:T(8,128)(2,1)S(1)}, bf16[200,1024]{1,0:T(8,128)(2,1)S(1)}, u32[]{:S(2)}, u32[]{:S(2)}) collective-permute-start(bf16[200,1024]{1,0:T(8,128)(2,1)S(1)} %reshape.186), channel_id=1, source_target_pairs={{0,56},{8,0},{16,8},{24,16},{32,24},{40,32},{48,40},{56,48},{1,57}... | collective-permute-start | bytes 1228808 | tf_op jit(solution)/shard_map/ppermute | solution.py:21
  23.5 11.4 %collective-permute-done.10 = bf16[200,1024]{1,0:T(8,128)(2,1)S(1)} collective-permute-done((bf16[200,1024]{1,0:T(8,128)(2,1)S(1)}, bf16[200,1024]{1,0:T(8,128)(2,1)S(1)}, u32[]{:S(2)}, u32[]{:S(2)}) %collective-permute-start.10) | collective-permute-done | bytes 409632 | tf_op jit(solution)/shard_map/ppermute | solution.py:21
  34.9 3.5 %collective-permute-start.12 = (bf16[200,1024]{1,0:T(8,128)(2,1)S(1)}, bf16[200,1024]{1,0:T(8,128)(2,1)S(1)}, u32[]{:S(2)}, u32[]{:S(2)}) collective-permute-start(bf16[200,1024]{1,0:T(8,128)(2,1)S(1)} %collective-permute-done.10), channel_id=1, source_target_pairs={{0,56},{8,0},{16,8},{24,16},{32,24},{40,32},{48,40},{56,48},{1,57}... | collective-permute-start | bytes 1228808 | tf_op jit(solution)/shard_map/ppermute | solution.py:21
  38.4 0.4 collective-permute-done.9
  39.1 0.5 fusion.2
  39.5 1.4 fusion.5
  41.0 4.3 %all-to-all-start.1 = ((bf16[4,2,64,2,400]{4,2,3,1,0:T(8,128)(2,1)}), bf16[4,2,64,2,400]{4,2,3,1,0:T(8,128)(2,1)S(1)}, u32[]{:S(2)}, u32[]{:S(2)}) async-start(bf16[4,2,64,2,400]{4,2,3,1,0:T(8,128)(2,1)} %bitcast.9), calls=%async_computation.1 | async-start | bytes 2097152 | tf_op jit(solution)/shard_map/all_to_all | solution.py:29
  45.7 9.5 %collective-permute-done.12 = bf16[200,1024]{1,0:T(8,128)(2,1)S(1)} collective-permute-done((bf16[200,1024]{1,0:T(8,128)(2,1)S(1)}, bf16[200,1024]{1,0:T(8,128)(2,1)S(1)}, u32[]{:S(2)}, u32[]{:S(2)}) %collective-permute-start.12) | collective-permute-done | bytes 409632 | tf_op jit(solution)/shard_map/ppermute | solution.py:21
  55.2 3.5 %collective-permute-start.14 = (bf16[200,1024]{1,0:T(8,128)(2,1)S(1)}, bf16[200,1024]{1,0:T(8,128)(2,1)S(1)}, u32[]{:S(2)}, u32[]{:S(2)}) collective-permute-start(bf16[200,1024]{1,0:T(8,128)(2,1)S(1)} %collective-permute-done.12), channel_id=1, source_target_pairs={{0,56},{8,0},{16,8},{24,16},{32,24},{40,32},{48,40},{56,48},{1,57}... | collective-permute-start | bytes 1228808 | tf_op jit(solution)/shard_map/ppermute | solution.py:21
  58.9 0.7 fusion.51
  59.6 1.9 iota_compare_fusion
  61.5 1.8 iota_compare_fusion.2
  63.4 2.0 collective-permute-done.14
  65.3 0.7 slice.93
  66.1 3.4 %collective-permute-start.16 = (bf16[104,1024]{1,0:T(8,128)(2,1)}, bf16[104,1024]{1,0:T(8,128)(2,1)}, u32[]{:S(2)}, u32[]{:S(2)}) collective-permute-start(bf16[104,1024]{1,0:T(8,128)(2,1)} %slice.93), channel_id=1, source_target_pairs={{0,56},{8,0},{16,8},{24,16},{32,24},{40,32},{48,40},{56,48},{1,57}... | collective-permute-start | bytes 638984 | tf_op jit(solution)/shard_map/ppermute | solution.py:21
  69.5 0.7 slice.92
  70.3 0.7 reshape.184
  71.1 1.1 copy.28
  72.2 0.7 reshape.185
  72.9 0.3 fusion.26
  73.2 0.3 fusion.21
  73.5 0.4 copy-done.12
  73.9 0.3 convolution_add_fusion.3
  74.2 0.3 convolution_add_fusion.2
  74.5 0.4 copy-done.14
  74.9 0.3 fusion.7
  75.2 0.7 copy-done.2
  75.9 0.3 fusion.18
  76.2 5.4 %collective-permute-done.15 = bf16[96,1024]{1,0:T(8,128)(2,1)} collective-permute-done((bf16[96,1024]{1,0:T(8,128)(2,1)}, bf16[96,1024]{1,0:T(8,128)(2,1)}, u32[]{:S(2)}, u32[]{:S(2)}) %collective-permute-start.15) | collective-permute-done | bytes 196640 | tf_op jit(solution)/shard_map/ppermute | solution.py:21
  81.6 1.3 fusion.10
  83.0 0.3 fusion.9
  83.5 3.0 %collective-permute-start.18 = (bf16[64,1024]{1,0:T(8,128)(2,1)S(1)}, bf16[64,1024]{1,0:T(8,128)(2,1)S(1)}, u32[]{:S(2)}, u32[]{:S(2)}) collective-permute-start(bf16[64,1024]{1,0:T(8,128)(2,1)S(1)} %get-tuple-element.9), channel_id=1, source_target_pairs={{0,128},{64,192},{128,0},{192,64},{1,129},{65,193},{129,1},{193,65... | collective-permute-start | bytes 393224 | tf_op jit(solution)/shard_map/ppermute | solution.py:25
  86.5 0.9 collective-permute-start.19
  87.3 1.3 iota_compare_fusion.4
  88.6 1.2 iota_compare_fusion.6
  89.9 0.8 collective-permute-done.17
  90.6 6.6 %collective-permute-done.18 = bf16[64,1024]{1,0:T(8,128)(2,1)S(1)} collective-permute-done((bf16[64,1024]{1,0:T(8,128)(2,1)S(1)}, bf16[64,1024]{1,0:T(8,128)(2,1)S(1)}, u32[]{:S(2)}, u32[]{:S(2)}) %collective-permute-start.18) | collective-permute-done | bytes 131104 | tf_op jit(solution)/shard_map/ppermute | solution.py:25
  97.3 1.2 select_select_fusion
  98.5 3.9 %all-to-all-start.2 = ((bf16[32,8,1024]{2,1,0:T(8,128)(2,1)}), bf16[32,8,1024]{2,1,0:T(8,128)(2,1)S(1)}, u32[]{:S(2)}, u32[]{:S(2)}) async-start(bf16[32,8,1024]{2,1,0:T(8,128)(2,1)} %select_select_fusion), calls=%async_computation.2 | async-start | bytes 1048576 | tf_op jit(solution)/shard_map/all_to_all | solution.py:29
  102.4 0.7 fusion.46
  103.2 0.6 fusion.48
  103.8 17.0 %all-to-all-done.2 = bf16[32,8,1024]{2,1,0:T(8,128)(2,1)S(1)} async-done(((bf16[32,8,1024]{2,1,0:T(8,128)(2,1)}), bf16[32,8,1024]{2,1,0:T(8,128)(2,1)S(1)}, u32[]{:S(2)}, u32[]{:S(2)}) %all-to-all-start.2) | async-done | bytes 524320 | tf_op jit(solution)/shard_map/all_to_all | solution.py:29
  120.8 0.6 gather_fusion
  121.3 1.1 broadcast_in_dim.149
  122.4 3.6 %all-to-all-start.3 = ((bf16[4,128,1024]{2,1,0:T(8,128)(2,1)}), bf16[4,128,1024]{2,1,0:T(8,128)(2,1)S(1)}, u32[]{:S(2)}, u32[]{:S(2)}) async-start(bf16[4,128,1024]{2,1,0:T(8,128)(2,1)} %broadcast_in_dim.149), calls=%async_computation.3 | async-start | bytes 2097152 | tf_op jit(solution)/shard_map/all_to_all | solution.py:29
  126.1 1.4 collective-permute-start.1
  127.5 1.3 collective-permute-start.3
  128.8 8.2 %collective-permute-start = (bf16[384,1024]{1,0:T(8,128)(2,1)S(1)}, bf16[384,1024]{1,0:T(8,128)(2,1)}, u32[]{:S(2)}, u32[]{:S(2)}) collective-permute-start(bf16[384,1024]{1,0:T(8,128)(2,1)S(1)} %bitcast.79), channel_id=1, source_target_pairs={{0,1},{1,0},{2,3},{3,2},{4,5},{5,4},{6,7},{7,6},{8,9},{9,8},{10,11... | collective-permute-start | bytes 2359304 | tf_op jit(solution)/shard_map/ppermute | solution.py:21
  137.1 13.1 %collective-permute-start.20 = (bf16[4,128,1024]{2,1,0:T(8,128)(2,1)S(1)}, bf16[4,128,1024]{2,1,0:T(8,128)(2,1)}, u32[]{:S(2)}, u32[]{:S(2)}) collective-permute-start(bf16[4,128,1024]{2,1,0:T(8,128)(2,1)S(1)} %all-to-all-done.3.refs_10_), channel_id=1, source_target_pairs={{0,1},{1,0},{2,3},{3,2},{4,5},{5,4},{6,7},{7,6},{8,9},{9,8},{10,11... | collective-permute-start | bytes 3145736 | tf_op jit(solution)/shard_map/ppermute | solution.py:21
  150.2 2.9 %collective-permute-done.1.refs_2_ = bf16[384,1024]{1,0:T(8,128)(2,1)} collective-permute-done((bf16[384,1024]{1,0:T(8,128)(2,1)S(1)}, bf16[384,1024]{1,0:T(8,128)(2,1)}, u32[]{:S(2)}, u32[]{:S(2)}) %collective-permute-start.1) | collective-permute-done | bytes 786464 | tf_op jit(solution)/shard_map/ppermute | solution.py:21
  153.1 1.0 slice.90
  154.2 1.0 slice.91
  155.2 2.7 %collective-permute-start.7 = (bf16[192,1024]{1,0:T(8,128)(2,1)S(1)}, bf16[192,1024]{1,0:T(8,128)(2,1)S(1)}, u32[]{:S(2)}, u32[]{:S(2)}) collective-permute-start(bf16[192,1024]{1,0:T(8,128)(2,1)S(1)} %slice.91), channel_id=1, source_target_pairs={{0,6},{2,0},{4,2},{6,4},{1,7},{3,1},{5,3},{7,5},{8,14},{10,8},{12,... | collective-permute-start | bytes 1179656 | tf_op jit(solution)/shard_map/ppermute | solution.py:21
  158.0 6.5 %collective-permute-start.2 = (bf16[384,1024]{1,0:T(8,128)(2,1)}, bf16[384,1024]{1,0:T(8,128)(2,1)}, u32[]{:S(2)}, u32[]{:S(2)}) collective-permute-start(bf16[384,1024]{1,0:T(8,128)(2,1)} %collective-permute-done.1.refs_2_), channel_id=1, source_target_pairs={{0,1},{1,0},{2,3},{3,2},{4,5},{5,4},{6,7},{7,6},{8,9},{9,8},{10,11... | collective-permute-start | bytes 2359304 | tf_op jit(solution)/shard_map/ppermute | solution.py:21
  165.8 3.3 %collective-permute-start.6 = (bf16[192,1024]{1,0:T(8,128)(2,1)S(1)}, bf16[192,1024]{1,0:T(8,128)(2,1)S(1)}, u32[]{:S(2)}, u32[]{:S(2)}) collective-permute-start(bf16[192,1024]{1,0:T(8,128)(2,1)S(1)} %collective-permute-done.5.refs_6_), channel_id=1, source_target_pairs={{0,1},{1,0},{2,3},{3,2},{4,5},{5,4},{6,7},{7,6},{8,9},{9,8},{10,11... | collective-permute-start | bytes 1179656 | tf_op jit(solution)/shard_map/ppermute | solution.py:21
  169.1 0.7 collective-permute-start.8
  169.9 0.8 fusion.36
  170.9 0.3 collective-permute-done.8.refs_9_
  171.2 19.4 %decoder.1 = bf16[384,512]{1,0:T(8,128)(2,1)} custom-call(s32[4]{0:T(128)S(1)} %pad_add_fusion.where_ref, bf16[384,1024]{1,0:T(8,128)(2,1)} %bitcast.76, bf16[384,1024]{1,0:T(8,128)(2,1)} %collective-permute-done.refs_1_, bf16[384,1024]{1,0:T(8,128)(2,1)} %collective-permute-done.1.refs_2_, bf16[384,1024]{1,0:T(8,128)(2,1)} %collective-permute-done.2.refs_3_, ...), custom_call_target="tpu_custom_call" | custom-call | tf_op jit(solution)/shard_map/decoder/pallas_call | solution.py:140
  (97 shorter events, 2.1 us)
Async XLA Ops:
  6.5 164.6 %all-gather.2.cloned.1.call-start = ((), (), s32[]{:S(2)}) async-start(), calls=%async_computation.4 | async-start | bytes 12976128 | tf_op jit(solution)/shard_map/all_gather | solution.py:196
  9.2 8.9 %copy-start.6 = (bf16[100,2,1024]{2,1,0:T(2,128)(2,1)S(1)}, bf16[100,2,1024]{2,1,0:T(2,128)(2,1)}, u32[]{:S(2)}) copy-start(bf16[100,2,1024]{2,1,0:T(2,128)(2,1)} %param.13) | copy-start | bytes 1228804
  11.3 11.9 %copy-start.16 = (f32[2,3200]{1,0:T(2,128)S(1)}, f32[2,3200]{1,0:T(2,128)}, u32[]{:S(2)}) copy-start(f32[2,3200]{1,0:T(2,128)} %param.11) | copy-start | bytes 76804
  11.3 12.1 %copy-start.17 = (f32[2,3200]{1,0:T(2,128)S(1)}, f32[2,3200]{1,0:T(2,128)}, u32[]{:S(2)}) copy-start(f32[2,3200]{1,0:T(2,128)} %param.12) | copy-start | bytes 76804
  11.3 27.5 %all-to-all-start = ((bf16[8,64,2,400]{3,1,2,0:T(8,128)(2,1)}), bf16[8,64,2,400]{3,1,2,0:T(8,128)(2,1)S(1)}, u32[]{:S(2)}, u32[]{:S(2)}) async-start(bf16[8,64,2,400]{3,1,2,0:T(8,128)(2,1)} %broadcast_in_dim.131), calls=%async_computation | async-start | bytes 2097152 | tf_op jit(solution)/shard_map/all_to_all | solution.py:29
  18.2 16.6 %collective-permute-start.10 = (bf16[200,1024]{1,0:T(8,128)(2,1)S(1)}, bf16[200,1024]{1,0:T(8,128)(2,1)S(1)}, u32[]{:S(2)}, u32[]{:S(2)}) collective-permute-start(bf16[200,1024]{1,0:T(8,128)(2,1)S(1)} %reshape.186), channel_id=1, source_target_pairs={{0,56},{8,0},{16,8},{24,16},{32,24},{40,32},{48,40},{56,48},{1,57}... | collective-permute-start | bytes 1228808 | tf_op jit(solution)/shard_map/ppermute | solution.py:21
  23.2 15.6 %collective-permute-start.9 = (bf16[200,1024]{1,0:T(8,128)(2,1)S(1)}, bf16[200,1024]{1,0:T(8,128)(2,1)S(1)}, u32[]{:S(2)}, u32[]{:S(2)}) collective-permute-start(bf16[200,1024]{1,0:T(8,128)(2,1)S(1)} %reshape.186), channel_id=1, source_target_pairs={{0,8},{8,16},{16,24},{24,32},{32,40},{40,48},{48,56},{56,0},{1,9},... | collective-permute-start | bytes 1228808 | tf_op jit(solution)/shard_map/ppermute | solution.py:21
  34.9 6.1 %copy-start.9 = (bf16[200,1024]{1,0:T(8,128)(2,1)}, bf16[200,1024]{1,0:T(8,128)(2,1)S(1)}, u32[]{:S(2)}) copy-start(bf16[200,1024]{1,0:T(8,128)(2,1)S(1)} %collective-permute-done.10) | copy-start | bytes 1228804
  34.9 20.3 %collective-permute-start.12 = (bf16[200,1024]{1,0:T(8,128)(2,1)S(1)}, bf16[200,1024]{1,0:T(8,128)(2,1)S(1)}, u32[]{:S(2)}, u32[]{:S(2)}) collective-permute-start(bf16[200,1024]{1,0:T(8,128)(2,1)S(1)} %collective-permute-done.10), channel_id=1, source_target_pairs={{0,56},{8,0},{16,8},{24,16},{32,24},{40,32},{48,40},{56,48},{1,57}... | collective-permute-start | bytes 1228808 | tf_op jit(solution)/shard_map/ppermute | solution.py:21
  38.8 2.2 %copy-start.11 = (bf16[200,1024]{1,0:T(8,128)(2,1)}, bf16[200,1024]{1,0:T(8,128)(2,1)S(1)}, u32[]{:S(2)}) copy-start(bf16[200,1024]{1,0:T(8,128)(2,1)S(1)} %collective-permute-done.9) | copy-start | bytes 1228804
  38.8 20.0 %collective-permute-start.11 = (bf16[200,1024]{1,0:T(8,128)(2,1)S(1)}, bf16[200,1024]{1,0:T(8,128)(2,1)S(1)}, u32[]{:S(2)}, u32[]{:S(2)}) collective-permute-start(bf16[200,1024]{1,0:T(8,128)(2,1)S(1)} %collective-permute-done.9), channel_id=1, source_target_pairs={{0,8},{8,16},{16,24},{24,32},{32,40},{40,48},{48,56},{56,0},{1,9},... | collective-permute-start | bytes 1228808 | tf_op jit(solution)/shard_map/ppermute | solution.py:21
  39.5 5.8 %copy-start.22 = (s32[32]{0:T(128)S(1)}, s32[32]{0:T(128)}, u32[]{:S(2)}) copy-start(s32[32]{0:T(128)} %param.18) | copy-start | bytes 388
  41.0 29.3 %all-to-all-start.1 = ((bf16[4,2,64,2,400]{4,2,3,1,0:T(8,128)(2,1)}), bf16[4,2,64,2,400]{4,2,3,1,0:T(8,128)(2,1)S(1)}, u32[]{:S(2)}, u32[]{:S(2)}) async-start(bf16[4,2,64,2,400]{4,2,3,1,0:T(8,128)(2,1)} %bitcast.9), calls=%async_computation.1 | async-start | bytes 2097152 | tf_op jit(solution)/shard_map/all_to_all | solution.py:29
  45.6 25.4 %copy-start.24 = (s32[32]{0:T(128)}, s32[32]{0:T(128)S(1)}, u32[]{:S(2)}) copy-start(s32[32]{0:T(128)S(1)} %reduce) | copy-start | bytes 388
  55.2 15.0 %copy-start.7 = (bf16[200,1024]{1,0:T(8,128)(2,1)}, bf16[200,1024]{1,0:T(8,128)(2,1)S(1)}, u32[]{:S(2)}) copy-start(bf16[200,1024]{1,0:T(8,128)(2,1)S(1)} %collective-permute-done.12) | copy-start | bytes 1228804
  55.2 10.1 %collective-permute-start.14 = (bf16[200,1024]{1,0:T(8,128)(2,1)S(1)}, bf16[200,1024]{1,0:T(8,128)(2,1)S(1)}, u32[]{:S(2)}, u32[]{:S(2)}) collective-permute-start(bf16[200,1024]{1,0:T(8,128)(2,1)S(1)} %collective-permute-done.12), channel_id=1, source_target_pairs={{0,56},{8,0},{16,8},{24,16},{32,24},{40,32},{48,40},{56,48},{1,57}... | collective-permute-start | bytes 1228808 | tf_op jit(solution)/shard_map/ppermute | solution.py:21
  58.7 12.3 %copy-start.13 = (bf16[200,1024]{1,0:T(8,128)(2,1)}, bf16[200,1024]{1,0:T(8,128)(2,1)S(1)}, u32[]{:S(2)}) copy-start(bf16[200,1024]{1,0:T(8,128)(2,1)S(1)} %collective-permute-done.11) | copy-start | bytes 1228804
  58.7 10.7 %collective-permute-start.13 = (bf16[200,1024]{1,0:T(8,128)(2,1)S(1)}, bf16[200,1024]{1,0:T(8,128)(2,1)S(1)}, u32[]{:S(2)}, u32[]{:S(2)}) collective-permute-start(bf16[200,1024]{1,0:T(8,128)(2,1)S(1)} %collective-permute-done.11), channel_id=1, source_target_pairs={{0,8},{8,16},{16,24},{24,32},{32,40},{40,48},{48,56},{56,0},{1,9},... | collective-permute-start | bytes 1228808 | tf_op jit(solution)/shard_map/ppermute | solution.py:21
  65.3 4.9 %copy-start.1 = (bf16[200,1024]{1,0:T(8,128)(2,1)}, bf16[200,1024]{1,0:T(8,128)(2,1)S(1)}, u32[]{:S(2)}) copy-start(bf16[200,1024]{1,0:T(8,128)(2,1)S(1)} %collective-permute-done.14) | copy-start | bytes 1228804
  66.1 15.6 %collective-permute-start.16 = (bf16[104,1024]{1,0:T(8,128)(2,1)}, bf16[104,1024]{1,0:T(8,128)(2,1)}, u32[]{:S(2)}, u32[]{:S(2)}) collective-permute-start(bf16[104,1024]{1,0:T(8,128)(2,1)} %slice.93), channel_id=1, source_target_pairs={{0,56},{8,0},{16,8},{24,16},{32,24},{40,32},{48,40},{56,48},{1,57}... | collective-permute-start | bytes 638984 | tf_op jit(solution)/shard_map/ppermute | solution.py:21
  69.5 0.9 copy-start.3
  70.2 11.4 %collective-permute-start.15 = (bf16[96,1024]{1,0:T(8,128)(2,1)}, bf16[96,1024]{1,0:T(8,128)(2,1)}, u32[]{:S(2)}, u32[]{:S(2)}) collective-permute-start(bf16[96,1024]{1,0:T(8,128)(2,1)} %slice.92), channel_id=1, source_target_pairs={{0,8},{8,16},{16,24},{24,32},{32,40},{40,48},{48,56},{56,0},{1,9},... | collective-permute-start | bytes 589832 | tf_op jit(solution)/shard_map/ppermute | solution.py:21
  72.2 1.0 copy-start.8
  72.9 1.0 copy-start.12
  73.2 1.0 copy-start.10
  73.9 1.0 copy-start.14
  74.9 1.0 copy-start.2
  75.9 7.0 %copy-start.4 = (bf16[200,1024]{1,0:T(8,128)(2,1)S(1)}, bf16[200,1024]{1,0:T(8,128)(2,1)}, u32[]{:S(2)}) copy-start(bf16[200,1024]{1,0:T(8,128)(2,1)} %copy-done.3) | copy-start | bytes 1228804
  83.0 14.3 %copy-start.18 = (pred[32]{0:T(512)(128)(4,1)S(1)}, pred[32]{0:T(512)(128)(4,1)}, u32[]{:S(2)}) copy-start(pred[32]{0:T(512)(128)(4,1)} %get-tuple-element.29) | copy-start | bytes 100
  83.0 14.3 %copy-start.19 = (pred[32]{0:T(512)(128)(4,1)S(1)}, pred[32]{0:T(512)(128)(4,1)}, u32[]{:S(2)}) copy-start(pred[32]{0:T(512)(128)(4,1)} %get-tuple-element.30) | copy-start | bytes 100
  83.0 14.3 %copy-start.20 = (pred[32]{0:T(512)(128)(4,1)S(1)}, pred[32]{0:T(512)(128)(4,1)}, u32[]{:S(2)}) copy-start(pred[32]{0:T(512)(128)(4,1)} %get-tuple-element.31) | copy-start | bytes 100
  83.0 14.3 %copy-start.21 = (pred[32]{0:T(512)(128)(4,1)S(1)}, pred[32]{0:T(512)(128)(4,1)}, u32[]{:S(2)}) copy-start(pred[32]{0:T(512)(128)(4,1)} %get-tuple-element.32) | copy-start | bytes 100
  83.3 19.1 %copy-start.23 = (s32[32]{0:T(128)S(1)}, s32[32]{0:T(128)}, u32[]{:S(2)}) copy-start(s32[32]{0:T(128)} %param.18) | copy-start | bytes 388
  83.3 19.1 %copy-start.25 = (s32[32]{0:T(128)S(1)}, s32[32]{0:T(128)}, u32[]{:S(2)}) copy-start(s32[32]{0:T(128)} %copy-done.24) | copy-start | bytes 388
  83.4 7.2 %collective-permute-start.17 = (bf16[64,1024]{1,0:T(8,128)(2,1)S(1)}, bf16[64,1024]{1,0:T(8,128)(2,1)S(1)}, u32[]{:S(2)}, u32[]{:S(2)}) collective-permute-start(bf16[64,1024]{1,0:T(8,128)(2,1)S(1)} %get-tuple-element.7), channel_id=1, source_target_pairs={{0,64},{64,0},{128,192},{192,128},{1,65},{65,1},{129,193},{193,129... | collective-permute-start | bytes 393224 | tf_op jit(solution)/shard_map/ppermute | solution.py:25
  83.5 13.7 %collective-permute-start.18 = (bf16[64,1024]{1,0:T(8,128)(2,1)S(1)}, bf16[64,1024]{1,0:T(8,128)(2,1)S(1)}, u32[]{:S(2)}, u32[]{:S(2)}) collective-permute-start(bf16[64,1024]{1,0:T(8,128)(2,1)S(1)} %get-tuple-element.9), channel_id=1, source_target_pairs={{0,128},{64,192},{128,0},{192,64},{1,129},{65,193},{129,1},{193,65... | collective-permute-start | bytes 393224 | tf_op jit(solution)/shard_map/ppermute | solution.py:25
  86.5 10.7 %collective-permute-start.19 = (bf16[64,1024]{1,0:T(8,128)(2,1)S(1)}, bf16[64,1024]{1,0:T(8,128)(2,1)S(1)}, u32[]{:S(2)}, u32[]{:S(2)}) collective-permute-start(bf16[64,1024]{1,0:T(8,128)(2,1)S(1)} %get-tuple-element.8), channel_id=1, source_target_pairs={{0,192},{64,128},{128,64},{192,0},{1,193},{65,129},{129,65},{193,1... | collective-permute-start | bytes 393224 | tf_op jit(solution)/shard_map/ppermute | solution.py:25
  98.5 22.2 %all-to-all-start.2 = ((bf16[32,8,1024]{2,1,0:T(8,128)(2,1)}), bf16[32,8,1024]{2,1,0:T(8,128)(2,1)S(1)}, u32[]{:S(2)}, u32[]{:S(2)}) async-start(bf16[32,8,1024]{2,1,0:T(8,128)(2,1)} %select_select_fusion), calls=%async_computation.2 | async-start | bytes 1048576 | tf_op jit(solution)/shard_map/all_to_all | solution.py:29
  102.4 23.6 %copy-start.5 = (bf16[1,384,1024]{2,1,0:T(8,128)(2,1)S(1)}, bf16[1,384,1024]{2,1,0:T(8,128)(2,1)}, u32[]{:S(2)}) copy-start(bf16[1,384,1024]{2,1,0:T(8,128)(2,1)} %param.14) | copy-start | bytes 2359300
  122.4 47.5 %copy-start.15 = (f32[8192]{0:T(1024)S(1)}, f32[8192]{0:T(1024)}, u32[]{:S(2)}) copy-start(f32[8192]{0:T(1024)} %param.15) | copy-start | bytes 98308
  122.4 14.6 %all-to-all-start.3 = ((bf16[4,128,1024]{2,1,0:T(8,128)(2,1)}), bf16[4,128,1024]{2,1,0:T(8,128)(2,1)S(1)}, u32[]{:S(2)}, u32[]{:S(2)}) async-start(bf16[4,128,1024]{2,1,0:T(8,128)(2,1)} %broadcast_in_dim.149), calls=%async_computation.3 | async-start | bytes 2097152 | tf_op jit(solution)/shard_map/all_to_all | solution.py:29
  126.1 27.0 %collective-permute-start.1 = (bf16[384,1024]{1,0:T(8,128)(2,1)S(1)}, bf16[384,1024]{1,0:T(8,128)(2,1)}, u32[]{:S(2)}, u32[]{:S(2)}) collective-permute-start(bf16[384,1024]{1,0:T(8,128)(2,1)S(1)} %bitcast.77), channel_id=1, source_target_pairs={{0,2},{2,4},{4,6},{6,0},{1,3},{3,5},{5,7},{7,1},{8,10},{10,12},{12... | collective-permute-start | bytes 2359304 | tf_op jit(solution)/shard_map/ppermute | solution.py:21
  127.5 26.7 %collective-permute-start.3 = (bf16[384,1024]{1,0:T(8,128)(2,1)S(1)}, bf16[384,1024]{1,0:T(8,128)(2,1)}, u32[]{:S(2)}, u32[]{:S(2)}) collective-permute-start(bf16[384,1024]{1,0:T(8,128)(2,1)S(1)} %bitcast.78), channel_id=1, source_target_pairs={{0,6},{2,0},{4,2},{6,4},{1,7},{3,1},{5,3},{7,5},{8,14},{10,8},{12,... | collective-permute-start | bytes 2359304 | tf_op jit(solution)/shard_map/ppermute | solution.py:21
  128.8 35.7 %collective-permute-start = (bf16[384,1024]{1,0:T(8,128)(2,1)S(1)}, bf16[384,1024]{1,0:T(8,128)(2,1)}, u32[]{:S(2)}, u32[]{:S(2)}) collective-permute-start(bf16[384,1024]{1,0:T(8,128)(2,1)S(1)} %bitcast.79), channel_id=1, source_target_pairs={{0,1},{1,0},{2,3},{3,2},{4,5},{5,4},{6,7},{7,6},{8,9},{9,8},{10,11... | collective-permute-start | bytes 2359304 | tf_op jit(solution)/shard_map/ppermute | solution.py:21
  137.1 34.1 %copy-start = (bf16[4,128,1024]{2,1,0:T(8,128)(2,1)}, bf16[4,128,1024]{2,1,0:T(8,128)(2,1)S(1)}, u32[]{:S(2)}) copy-start(bf16[4,128,1024]{2,1,0:T(8,128)(2,1)S(1)} %all-to-all-done.3.refs_10_) | copy-start | bytes 3145732
  137.1 34.1 %collective-permute-start.20 = (bf16[4,128,1024]{2,1,0:T(8,128)(2,1)S(1)}, bf16[4,128,1024]{2,1,0:T(8,128)(2,1)}, u32[]{:S(2)}, u32[]{:S(2)}) collective-permute-start(bf16[4,128,1024]{2,1,0:T(8,128)(2,1)S(1)} %all-to-all-done.3.refs_10_), channel_id=1, source_target_pairs={{0,1},{1,0},{2,3},{3,2},{4,5},{5,4},{6,7},{7,6},{8,9},{9,8},{10,11... | collective-permute-start | bytes 3145736 | tf_op jit(solution)/shard_map/ppermute | solution.py:21
  154.1 11.7 %collective-permute-start.5 = (bf16[192,1024]{1,0:T(8,128)(2,1)S(1)}, bf16[192,1024]{1,0:T(8,128)(2,1)S(1)}, u32[]{:S(2)}, u32[]{:S(2)}) collective-permute-start(bf16[192,1024]{1,0:T(8,128)(2,1)S(1)} %slice.90), channel_id=1, source_target_pairs={{0,2},{2,4},{4,6},{6,0},{1,3},{3,5},{5,7},{7,1},{8,10},{10,12},{12... | collective-permute-start | bytes 1179656 | tf_op jit(solution)/shard_map/ppermute | solution.py:21
  155.2 13.9 %collective-permute-start.7 = (bf16[192,1024]{1,0:T(8,128)(2,1)S(1)}, bf16[192,1024]{1,0:T(8,128)(2,1)S(1)}, u32[]{:S(2)}, u32[]{:S(2)}) collective-permute-start(bf16[192,1024]{1,0:T(8,128)(2,1)S(1)} %slice.91), channel_id=1, source_target_pairs={{0,6},{2,0},{4,2},{6,4},{1,7},{3,1},{5,3},{7,5},{8,14},{10,8},{12,... | collective-permute-start | bytes 1179656 | tf_op jit(solution)/shard_map/ppermute | solution.py:21
  158.0 13.2 %collective-permute-start.2 = (bf16[384,1024]{1,0:T(8,128)(2,1)}, bf16[384,1024]{1,0:T(8,128)(2,1)}, u32[]{:S(2)}, u32[]{:S(2)}) collective-permute-start(bf16[384,1024]{1,0:T(8,128)(2,1)} %collective-permute-done.1.refs_2_), channel_id=1, source_target_pairs={{0,1},{1,0},{2,3},{3,2},{4,5},{5,4},{6,7},{7,6},{8,9},{9,8},{10,11... | collective-permute-start | bytes 2359304 | tf_op jit(solution)/shard_map/ppermute | solution.py:21
  164.5 6.6 %collective-permute-start.4 = (bf16[384,1024]{1,0:T(8,128)(2,1)}, bf16[384,1024]{1,0:T(8,128)(2,1)}, u32[]{:S(2)}, u32[]{:S(2)}) collective-permute-start(bf16[384,1024]{1,0:T(8,128)(2,1)} %collective-permute-done.3.refs_4_), channel_id=1, source_target_pairs={{0,1},{1,0},{2,3},{3,2},{4,5},{5,4},{6,7},{7,6},{8,9},{9,8},{10,11... | collective-permute-start | bytes 2359304 | tf_op jit(solution)/shard_map/ppermute | solution.py:21
  165.8 5.0 %collective-permute-start.6 = (bf16[192,1024]{1,0:T(8,128)(2,1)S(1)}, bf16[192,1024]{1,0:T(8,128)(2,1)S(1)}, u32[]{:S(2)}, u32[]{:S(2)}) collective-permute-start(bf16[192,1024]{1,0:T(8,128)(2,1)S(1)} %collective-permute-done.5.refs_6_), channel_id=1, source_target_pairs={{0,1},{1,0},{2,3},{3,2},{4,5},{5,4},{6,7},{7,6},{8,9},{9,8},{10,11... | collective-permute-start | bytes 1179656 | tf_op jit(solution)/shard_map/ppermute | solution.py:21
  169.1 2.0 %collective-permute-start.8 = (bf16[192,1024]{1,0:T(8,128)(2,1)S(1)}, bf16[192,1024]{1,0:T(8,128)(2,1)S(1)}, u32[]{:S(2)}, u32[]{:S(2)}) collective-permute-start(bf16[192,1024]{1,0:T(8,128)(2,1)S(1)} %collective-permute-done.7.refs_8_), channel_id=1, source_target_pairs={{0,1},{1,0},{2,3},{3,2},{4,5},{5,4},{6,7},{7,6},{8,9},{9,8},{10,11... | collective-permute-start | bytes 1179656 | tf_op jit(solution)/shard_map/ppermute | solution.py:21
Sparse Core Ops, SparseCore 0:
  9.9 136.9 all-gather.1
where the time goes:
time: 199 us; the launch traced here: 197 us
  starting transfers between devices  75.4 us (38%)
  waiting for transfers between devices  56.2 us (28%)
  Pallas kernels  19.4 us (10%)
  between operations  15.3 us (8%)
  other arithmetic  14.2 us (7%)
  local copies, waits for them, and re-layouts  13.6 us (7%)
  matrix products  3.39 us (2%)
    ppermute x18, starting transfers between devices, shift(): lax.ppermute(array, axis, [(i, (i + by) % size) for i in range(size)])  52.8 us
    ppermute x18, waiting for transfers between devices, shift(): lax.ppermute(array, axis, [(i, (i + by) % size) for i in range(size)])  31.9 us
    pallas_call x1, Pallas kernels, decoder(): pl.pallas_call(kernel, out_shape=jax.ShapeDtypeStruct((SEQ, 512), jnp.bfl...  19.4 us
    all_to_all x4, starting transfers between devices, exchange(): return lax.all_to_all(array, axis, 0, 0, tiled=True)  18.7 us
    all_to_all x4, waiting for transfers between devices, exchange(): return lax.all_to_all(array, axis, 0, 0, tiled=True)  17 us
    ppermute x3, waiting for transfers between devices, flip_x(): return lax.ppermute(array, 'x', [(i, i ^ flip) for i in range(NX)])  7.33 us
    eq x4, other arithmetic, step(): owners[r] == sample_ids  6.25 us
  transfers between devices with their start and end apart: 26, of which 10 were waited for; matrix products, arithmetic and copies ran while one was open for 14% of the time, Pallas kernels for 0%

commit v1 on v0

--- a/solution.py
+++ b/solution.py
@@ -76,17 +76,12 @@
     return (value * cos + pltpu.roll(value, 64, 1) * sin).astype(jnp.bfloat16)
 
 
-def decoder(where, text, image, gain, weight, cosine, sine):
+def prepare(where, text, image, gain):
     arrays = [a for a, _, _, _ in text] + list(image)
     n_text, count = len(text), len(arrays)
 
     def kernel(where_ref, *refs):
-        gain_ref, w_hbm, cos_ref, sin_ref, out_ref, a_ref, w_ref, w_sem = refs[count:]
-        loads = []
-        for t in range(8):
-            rows = pl.ds(t * 1024, 1024)
-            loads.append(pltpu.make_async_copy(w_hbm.at[rows, :], w_ref.at[rows, :], w_sem.at[t]))
-            loads[-1].start()
+        gain_ref, a_ref = refs[count:]
         y, c = where_ref[0], where_ref[1]
         start, n_rows = where_ref[2], where_ref[3]
         total = None
@@ -110,14 +105,42 @@
                 squares = jnp.concatenate([squares, zero] if first == 0 else [zero, squares], axis=0)
             total = squares if total is None else total + squares
         scale = lax.rsqrt(total * (1.0 / WIDTH) + decoder_epsilon)
+        for t in range(8):
+            a_ref[t] = (
+                a_ref[t].astype(jnp.float32) * scale * gain_ref[t : t + 1, :]
+            ).astype(jnp.bfloat16)
+
+    return pl.pallas_call(
+        kernel,
+        out_shape=jax.ShapeDtypeStruct((8, SEQ, 1024), jnp.bfloat16),
+        in_specs=[SMEM] + [VMEM] * (count + 1),
+        out_specs=VMEM,
+        compiler_params=pltpu.CompilerParams(vmem_limit_bytes=48 * 1024 * 1024),
+        name="prepare",
+    )(where, *arrays, gain)
+
+
+def attention(sequence, weight, cosine, sine):
+    def kernel(
+        a_hbm, w_hbm, cos_ref, sin_ref, out_ref, a_ref, w_ref, a_sem, w_sem
+    ):
+        loads = []
+        for t in range(8):
+            rows = pl.ds(t * 1024, 1024)
+            loads.append(
+                (
+                    pltpu.make_async_copy(a_hbm.at[t], a_ref.at[t], a_sem.at[t]),
+                    pltpu.make_async_copy(w_hbm.at[rows, :], w_ref.at[rows, :], w_sem.at[t]),
+                )
+            )
+            for copy in loads[-1]:
+                copy.start()
         acc = jnp.zeros((SEQ, 768), jnp.float32)
         for t in range(8):
-            normed = (
-                a_ref[t].astype(jnp.float32) * scale * gain_ref[t : t + 1, :]
-            ).astype(jnp.bfloat16)
-            loads[t].wait()
+            for copy in loads[t]:
+                copy.wait()
             acc = acc + jnp.dot(
-                normed, w_ref[t * 1024 : (t + 1) * 1024, :], preferred_element_type=jnp.float32
+                a_ref[t], w_ref[t * 1024 : (t + 1) * 1024, :], preferred_element_type=jnp.float32
             )
         cos, sin = cos_ref[...], sin_ref[...]
         key = rotated(acc[:, 512:640], cos, sin)
@@ -140,16 +163,17 @@
     return pl.pallas_call(
         kernel,
         out_shape=jax.ShapeDtypeStruct((SEQ, 512), jnp.bfloat16),
-        in_specs=[SMEM] + [VMEM] * (count + 1) + [HBM] + [VMEM] * 2,
+        in_specs=[HBM] * 2 + [VMEM] * 2,
         out_specs=VMEM,
         scratch_shapes=[
             pltpu.VMEM((8, SEQ, 1024), jnp.bfloat16),
             pltpu.VMEM((WIDTH, 768), jnp.bfloat16),
             pltpu.SemaphoreType.DMA((8,)),
+            pltpu.SemaphoreType.DMA((8,)),
         ],
-        compiler_params=pltpu.CompilerParams(vmem_limit_bytes=52 * 1024 * 1024),
-        name="decoder",
-    )(where, *arrays, gain, weight, cosine, sine)
+        compiler_params=pltpu.CompilerParams(vmem_limit_bytes=56 * 1024 * 1024),
+        name="attention",
+    )(sequence, weight, cosine, sine)
 
 
 def vision(vis_rows, ln_gain, ln_bias, proj_weight, z):
@@ -217,9 +241,8 @@
     rows = entry(tile_counts, place) * 8
     where = jnp.stack([y, c, image_offsets[0], rows]).astype(jnp.int32)
     cosine, sine = rope_tables()
-    gain = attn_gain.reshape(8, 1024)
-    out = decoder(where, text, (own_image, other_image), gain, both_all, cosine, sine)
-    return out[None]
+    sequence = prepare(where, text, (own_image, other_image), attn_gain.reshape(8, 1024))
+    return attention(sequence, both_all, cosine, sine)[None]
 
 
 def solution(mesh):

time: 199 us -> 206 us (1.035)
  Pallas kernels: 19.4 us -> 23 us
    pallas_call x1 -> x2, Pallas kernels: 19.4 us -> 23 us  [the longest x1 13.6 us: attention(): pl.pallas_call(kernel, out_shape=jax.ShapeDtypeStruct((SEQ, 512), jnp.bfl...]
  transfers between devices with their start and end apart: 26 -> 26, of which waited for: 10 -> 9; matrix products, arithmetic and copies ran while one was open for 14% -> 14% of each run, Pallas kernels for 0% -> 5%
where the time goes in v1:
time: 206 us; the launch traced here: 204 us
  starting transfers between devices  76.2 us (37%)
  waiting for transfers between devices  56.5 us (27%)
  Pallas kernels  23 us (11%)
  local copies, waits for them, and re-layouts  15.2 us (7%)
  between operations  15.2 us (7%)
  other arithmetic  14.9 us (7%)
  matrix products  3.39 us (2%)
    ppermute x18, starting transfers between devices, shift(): lax.ppermute(array, axis, [(i, (i + by) % size) for i in range(size)])  53 us
    ppermute x18, waiting for transfers between devices, shift(): lax.ppermute(array, axis, [(i, (i + by) % size) for i in range(size)])  31.5 us
    all_to_all x4, starting transfers between devices, exchange(): return lax.all_to_all(array, axis, 0, 0, tiled=True)  19.3 us
    all_to_all x4, waiting for transfers between devices, exchange(): return lax.all_to_all(array, axis, 0, 0, tiled=True)  17.1 us
    pallas_call x1, Pallas kernels, attention(): pl.pallas_call(kernel, out_shape=jax.ShapeDtypeStruct((SEQ, 512), jnp.bfl...  13.6 us
    pallas_call x1, Pallas kernels, prepare(): pl.pallas_call(kernel, out_shape=jax.ShapeDtypeStruct((8, SEQ, 1024), jnp...  9.45 us
    ppermute x3, waiting for transfers between devices, flip_x(): return lax.ppermute(array, 'x', [(i, i ^ flip) for i in range(NX)])  7.97 us
    eq x4, other arithmetic, step(): owners[r] == sample_ids  6.18 us
  transfers between devices with their start and end apart: 26, of which 9 were waited for; matrix products, arithmetic and copies ran while one was open for 14% of the time, Pallas kernels for 5%

profile of v1, /device:TPU:1, one launch (start us, length us, event | category | flops | bytes accessed | tf_op | source)
XLA Modules:
  0.0 204.5 jit_solution(526038039664668130)
XLA Ops:
  6.5 0.9 copy.32
  7.5 1.8 pad_maximum_fusion
  9.2 1.0 copy.25
  10.2 1.1 broadcast_in_dim.131
  11.3 6.8 %all-to-all-start = ((bf16[8,64,2,400]{3,1,2,0:T(8,128)(2,1)}), bf16[8,64,2,400]{3,1,2,0:T(8,128)(2,1)S(1)}, u32[]{:S(2)}, u32[]{:S(2)}) async-start(bf16[8,64,2,400]{3,1,2,0:T(8,128)(2,1)} %broadcast_in_dim.131), calls=%async_computation | async-start | bytes 2097152 | tf_op jit(solution)/shard_map/all_to_all | solution.py:29
  18.3 5.0 %collective-permute-start.10 = (bf16[200,1024]{1,0:T(8,128)(2,1)S(1)}, bf16[200,1024]{1,0:T(8,128)(2,1)S(1)}, u32[]{:S(2)}, u32[]{:S(2)}) collective-permute-start(bf16[200,1024]{1,0:T(8,128)(2,1)S(1)} %reshape.186), channel_id=1, source_target_pairs={{0,56},{8,0},{16,8},{24,16},{32,24},{40,32},{48,40},{56,48},{1,57}... | collective-permute-start | bytes 1228808 | tf_op jit(solution)/shard_map/ppermute | solution.py:21
  23.5 11.5 %collective-permute-done.10 = bf16[200,1024]{1,0:T(8,128)(2,1)S(1)} collective-permute-done((bf16[200,1024]{1,0:T(8,128)(2,1)S(1)}, bf16[200,1024]{1,0:T(8,128)(2,1)S(1)}, u32[]{:S(2)}, u32[]{:S(2)}) %collective-permute-start.10) | collective-permute-done | bytes 409632 | tf_op jit(solution)/shard_map/ppermute | solution.py:21
  35.0 3.5 %collective-permute-start.12 = (bf16[200,1024]{1,0:T(8,128)(2,1)S(1)}, bf16[200,1024]{1,0:T(8,128)(2,1)S(1)}, u32[]{:S(2)}, u32[]{:S(2)}) collective-permute-start(bf16[200,1024]{1,0:T(8,128)(2,1)S(1)} %collective-permute-done.10), channel_id=1, source_target_pairs={{0,56},{8,0},{16,8},{24,16},{32,24},{40,32},{48,40},{56,48},{1,57}... | collective-permute-start | bytes 1228808 | tf_op jit(solution)/shard_map/ppermute | solution.py:21
  38.5 0.4 collective-permute-done.9
  39.1 0.5 fusion.2
  39.6 1.5 fusion.5
  41.1 4.3 %all-to-all-start.1 = ((bf16[4,2,64,2,400]{4,2,3,1,0:T(8,128)(2,1)}), bf16[4,2,64,2,400]{4,2,3,1,0:T(8,128)(2,1)S(1)}, u32[]{:S(2)}, u32[]{:S(2)}) async-start(bf16[4,2,64,2,400]{4,2,3,1,0:T(8,128)(2,1)} %bitcast.9), calls=%async_computation.1 | async-start | bytes 2097152 | tf_op jit(solution)/shard_map/all_to_all | solution.py:29
  45.7 9.4 %collective-permute-done.12 = bf16[200,1024]{1,0:T(8,128)(2,1)S(1)} collective-permute-done((bf16[200,1024]{1,0:T(8,128)(2,1)S(1)}, bf16[200,1024]{1,0:T(8,128)(2,1)S(1)}, u32[]{:S(2)}, u32[]{:S(2)}) %collective-permute-start.12) | collective-permute-done | bytes 409632 | tf_op jit(solution)/shard_map/ppermute | solution.py:21
  55.2 3.5 %collective-permute-start.14 = (bf16[200,1024]{1,0:T(8,128)(2,1)S(1)}, bf16[200,1024]{1,0:T(8,128)(2,1)S(1)}, u32[]{:S(2)}, u32[]{:S(2)}) collective-permute-start(bf16[200,1024]{1,0:T(8,128)(2,1)S(1)} %collective-permute-done.12), channel_id=1, source_target_pairs={{0,56},{8,0},{16,8},{24,16},{32,24},{40,32},{48,40},{56,48},{1,57}... | collective-permute-start | bytes 1228808 | tf_op jit(solution)/shard_map/ppermute | solution.py:21
  58.9 0.7 fusion.51
  59.6 1.9 iota_compare_fusion
  61.4 1.9 iota_compare_fusion.2
  63.4 1.9 collective-permute-done.14
  65.3 0.7 slice.93
  66.0 3.4 %collective-permute-start.16 = (bf16[104,1024]{1,0:T(8,128)(2,1)}, bf16[104,1024]{1,0:T(8,128)(2,1)}, u32[]{:S(2)}, u32[]{:S(2)}) collective-permute-start(bf16[104,1024]{1,0:T(8,128)(2,1)} %slice.93), channel_id=1, source_target_pairs={{0,56},{8,0},{16,8},{24,16},{32,24},{40,32},{48,40},{56,48},{1,57}... | collective-permute-start | bytes 638984 | tf_op jit(solution)/shard_map/ppermute | solution.py:21
  69.4 0.7 slice.92
  70.3 0.7 reshape.184
  71.0 1.1 copy.28
  72.1 0.7 reshape.185
  73.1 0.3 fusion.21
  73.4 0.4 copy-done.12
  74.5 0.4 copy-done.14
  74.9 0.3 fusion.7
  75.2 0.7 copy-done.3
  76.2 5.4 %collective-permute-done.15 = bf16[96,1024]{1,0:T(8,128)(2,1)} collective-permute-done((bf16[96,1024]{1,0:T(8,128)(2,1)}, bf16[96,1024]{1,0:T(8,128)(2,1)}, u32[]{:S(2)}, u32[]{:S(2)}) %collective-permute-start.15) | collective-permute-done | bytes 196640 | tf_op jit(solution)/shard_map/ppermute | solution.py:21
  81.6 1.3 fusion.10
  82.9 0.3 fusion.9
  83.3 0.6 collective-permute-start.17
  83.9 2.9 %collective-permute-start.18 = (bf16[64,1024]{1,0:T(8,128)(2,1)S(1)}, bf16[64,1024]{1,0:T(8,128)(2,1)S(1)}, u32[]{:S(2)}, u32[]{:S(2)}) collective-permute-start(bf16[64,1024]{1,0:T(8,128)(2,1)S(1)} %get-tuple-element.9), channel_id=1, source_target_pairs={{0,128},{64,192},{128,0},{192,64},{1,129},{65,193},{129,1},{193,65... | collective-permute-start | bytes 393224 | tf_op jit(solution)/shard_map/ppermute | solution.py:25
  86.9 0.4 collective-permute-start.19
  87.3 1.2 iota_compare_fusion.4
  88.5 1.2 iota_compare_fusion.6
  89.7 0.9 collective-permute-done.17
  90.6 7.1 %collective-permute-done.18 = bf16[64,1024]{1,0:T(8,128)(2,1)S(1)} collective-permute-done((bf16[64,1024]{1,0:T(8,128)(2,1)S(1)}, bf16[64,1024]{1,0:T(8,128)(2,1)S(1)}, u32[]{:S(2)}, u32[]{:S(2)}) %collective-permute-start.18) | collective-permute-done | bytes 131104 | tf_op jit(solution)/shard_map/ppermute | solution.py:25
  97.8 1.2 select_select_fusion
  99.0 3.9 %all-to-all-start.2 = ((bf16[32,8,1024]{2,1,0:T(8,128)(2,1)}), bf16[32,8,1024]{2,1,0:T(8,128)(2,1)S(1)}, u32[]{:S(2)}, u32[]{:S(2)}) async-start(bf16[32,8,1024]{2,1,0:T(8,128)(2,1)} %select_select_fusion), calls=%async_computation.2 | async-start | bytes 1048576 | tf_op jit(solution)/shard_map/all_to_all | solution.py:29
  102.9 0.6 fusion.46
  103.5 0.7 fusion.48
  104.2 17.0 %all-to-all-done.2 = bf16[32,8,1024]{2,1,0:T(8,128)(2,1)S(1)} async-done(((bf16[32,8,1024]{2,1,0:T(8,128)(2,1)}), bf16[32,8,1024]{2,1,0:T(8,128)(2,1)S(1)}, u32[]{:S(2)}, u32[]{:S(2)}) %all-to-all-start.2) | async-done | bytes 524320 | tf_op jit(solution)/shard_map/all_to_all | solution.py:29
  121.3 0.6 gather_fusion
  121.8 1.1 broadcast_in_dim.149
  122.9 4.3 %all-to-all-start.3 = ((bf16[4,128,1024]{2,1,0:T(8,128)(2,1)}), bf16[4,128,1024]{2,1,0:T(8,128)(2,1)}, u32[]{:S(2)}, u32[]{:S(2)}) async-start(bf16[4,128,1024]{2,1,0:T(8,128)(2,1)} %broadcast_in_dim.149), calls=%async_computation.3 | async-start | bytes 2097152 | tf_op jit(solution)/shard_map/all_to_all | solution.py:29
  127.2 1.4 collective-permute-start.1
  128.6 1.3 collective-permute-start.3
  130.0 8.1 %collective-permute-start = (bf16[384,1024]{1,0:T(8,128)(2,1)S(1)}, bf16[384,1024]{1,0:T(8,128)(2,1)S(1)}, u32[]{:S(2)}, u32[]{:S(2)}) collective-permute-start(bf16[384,1024]{1,0:T(8,128)(2,1)S(1)} %bitcast.74), channel_id=1, source_target_pairs={{0,1},{1,0},{2,3},{3,2},{4,5},{5,4},{6,7},{7,6},{8,9},{9,8},{10,11... | collective-permute-start | bytes 2359304 | tf_op jit(solution)/shard_map/ppermute | solution.py:21
  138.1 13.2 %collective-permute-start.20 = (bf16[4,128,1024]{2,1,0:T(8,128)(2,1)}, bf16[4,128,1024]{2,1,0:T(8,128)(2,1)}, u32[]{:S(2)}, u32[]{:S(2)}) collective-permute-start(bf16[4,128,1024]{2,1,0:T(8,128)(2,1)} %all-to-all-done.3.refs_10_), channel_id=1, source_target_pairs={{0,1},{1,0},{2,3},{3,2},{4,5},{5,4},{6,7},{7,6},{8,9},{9,8},{10,11... | collective-permute-start | bytes 3145736 | tf_op jit(solution)/shard_map/ppermute | solution.py:21
  151.3 2.9 %collective-permute-done.1.refs_2_ = bf16[384,1024]{1,0:T(8,128)(2,1)S(1)} collective-permute-done((bf16[384,1024]{1,0:T(8,128)(2,1)S(1)}, bf16[384,1024]{1,0:T(8,128)(2,1)S(1)}, u32[]{:S(2)}, u32[]{:S(2)}) %collective-permute-start.1) | collective-permute-done | bytes 786464 | tf_op jit(solution)/shard_map/ppermute | solution.py:21
  154.2 0.8 slice.90
  155.0 0.8 slice.91
  155.8 2.7 %collective-permute-start.7 = (bf16[192,1024]{1,0:T(8,128)(2,1)}, bf16[192,1024]{1,0:T(8,128)(2,1)}, u32[]{:S(2)}, u32[]{:S(2)}) collective-permute-start(bf16[192,1024]{1,0:T(8,128)(2,1)} %slice.91), channel_id=1, source_target_pairs={{0,6},{2,0},{4,2},{6,4},{1,7},{3,1},{5,3},{7,5},{8,14},{10,8},{12,... | collective-permute-start | bytes 1179656 | tf_op jit(solution)/shard_map/ppermute | solution.py:21
  158.4 6.5 %collective-permute-start.2 = (bf16[384,1024]{1,0:T(8,128)(2,1)S(1)}, bf16[384,1024]{1,0:T(8,128)(2,1)}, u32[]{:S(2)}, u32[]{:S(2)}) collective-permute-start(bf16[384,1024]{1,0:T(8,128)(2,1)S(1)} %collective-permute-done.1.refs_2_), channel_id=1, source_target_pairs={{0,1},{1,0},{2,3},{3,2},{4,5},{5,4},{6,7},{7,6},{8,9},{9,8},{10,11... | collective-permute-start | bytes 2359304 | tf_op jit(solution)/shard_map/ppermute | solution.py:21
  166.3 3.9 %collective-permute-start.6 = (bf16[192,1024]{1,0:T(8,128)(2,1)S(1)}, bf16[192,1024]{1,0:T(8,128)(2,1)}, u32[]{:S(2)}, u32[]{:S(2)}) collective-permute-start(bf16[192,1024]{1,0:T(8,128)(2,1)S(1)} %collective-permute-done.5.refs_6_), channel_id=1, source_target_pairs={{0,1},{1,0},{2,3},{3,2},{4,5},{5,4},{6,7},{7,6},{8,9},{9,8},{10,11... | collective-permute-start | bytes 1179656 | tf_op jit(solution)/shard_map/ppermute | solution.py:21
  170.1 0.4 collective-permute-start.8
  170.7 1.4 reshape.188.refs_12_
  172.0 0.8 fusion.36
  172.8 1.0 pad_maximum_fusion.1
  173.8 0.7 copy-done.1
  174.6 9.5 %prepare.1.a_hbm = bf16[8,384,1024]{2,1,0:T(8,128)(2,1)} custom-call(s32[4]{0:T(128)S(1)} %pad_add_fusion.where_ref, bf16[384,1024]{1,0:T(8,128)(2,1)S(1)} %bitcast.75, bf16[384,1024]{1,0:T(8,128)(2,1)S(1)} %collective-permute-done.refs_1_, bf16[384,1024]{1,0:T(8,128)(2,1)S(1)} %collective-permute-done.1.refs_2_, ...), custom_call_target="tpu_custom_call" | custom-call | tf_op jit(solution)/shard_map/prepare/pallas_call | solution.py:113
  184.0 13.6 %attention.1 = bf16[384,512]{1,0:T(8,128)(2,1)} custom-call(bf16[8,384,1024]{2,1,0:T(8,128)(2,1)} %prepare.1.a_hbm, bf16[8192,768]{1,0:T(8,128)(2,1)} %all-gather.2.cloned.1.call-done.w_hbm, f32[384,128]{1,0:T(8,128)} %get-tuple-element.37.cos_ref, f32[384,128]{1,0:T(8,128)} %get-tuple-element.38.sin_ref), custom_call_target="tpu_custom_call" | custom-call | tf_op jit(solution)/shard_map/attention/pallas_call | solution.py:163
  (96 shorter events, 2.8 us)
Async XLA Ops:
  6.5 177.5 %all-gather.2.cloned.1.call-start = ((), (), s32[]{:S(2)}) async-start(), calls=%async_computation.4 | async-start | bytes 12976128 | tf_op jit(solution)/shard_map/all_gather | solution.py:220
  9.2 8.9 %copy-start.6 = (bf16[100,2,1024]{2,1,0:T(2,128)(2,1)S(1)}, bf16[100,2,1024]{2,1,0:T(2,128)(2,1)}, u32[]{:S(2)}) copy-start(bf16[100,2,1024]{2,1,0:T(2,128)(2,1)} %param.13) | copy-start | bytes 1228804
  11.3 11.9 %copy-start.15 = (f32[2,3200]{1,0:T(2,128)S(1)}, f32[2,3200]{1,0:T(2,128)}, u32[]{:S(2)}) copy-start(f32[2,3200]{1,0:T(2,128)} %param.11) | copy-start | bytes 76804
  11.3 12.1 %copy-start.16 = (f32[2,3200]{1,0:T(2,128)S(1)}, f32[2,3200]{1,0:T(2,128)}, u32[]{:S(2)}) copy-start(f32[2,3200]{1,0:T(2,128)} %param.12) | copy-start | bytes 76804
  11.3 27.6 %all-to-all-start = ((bf16[8,64,2,400]{3,1,2,0:T(8,128)(2,1)}), bf16[8,64,2,400]{3,1,2,0:T(8,128)(2,1)S(1)}, u32[]{:S(2)}, u32[]{:S(2)}) async-start(bf16[8,64,2,400]{3,1,2,0:T(8,128)(2,1)} %broadcast_in_dim.131), calls=%async_computation | async-start | bytes 2097152 | tf_op jit(solution)/shard_map/all_to_all | solution.py:29
  18.3 16.7 %collective-permute-start.10 = (bf16[200,1024]{1,0:T(8,128)(2,1)S(1)}, bf16[200,1024]{1,0:T(8,128)(2,1)S(1)}, u32[]{:S(2)}, u32[]{:S(2)}) collective-permute-start(bf16[200,1024]{1,0:T(8,128)(2,1)S(1)} %reshape.186), channel_id=1, source_target_pairs={{0,56},{8,0},{16,8},{24,16},{32,24},{40,32},{48,40},{56,48},{1,57}... | collective-permute-start | bytes 1228808 | tf_op jit(solution)/shard_map/ppermute | solution.py:21
  23.2 15.6 %collective-permute-start.9 = (bf16[200,1024]{1,0:T(8,128)(2,1)S(1)}, bf16[200,1024]{1,0:T(8,128)(2,1)S(1)}, u32[]{:S(2)}, u32[]{:S(2)}) collective-permute-start(bf16[200,1024]{1,0:T(8,128)(2,1)S(1)} %reshape.186), channel_id=1, source_target_pairs={{0,8},{8,16},{16,24},{24,32},{32,40},{40,48},{48,56},{56,0},{1,9},... | collective-permute-start | bytes 1228808 | tf_op jit(solution)/shard_map/ppermute | solution.py:21
  35.0 6.1 %copy-start.9 = (bf16[200,1024]{1,0:T(8,128)(2,1)}, bf16[200,1024]{1,0:T(8,128)(2,1)S(1)}, u32[]{:S(2)}) copy-start(bf16[200,1024]{1,0:T(8,128)(2,1)S(1)} %collective-permute-done.10) | copy-start | bytes 1228804
  35.0 20.2 %collective-permute-start.12 = (bf16[200,1024]{1,0:T(8,128)(2,1)S(1)}, bf16[200,1024]{1,0:T(8,128)(2,1)S(1)}, u32[]{:S(2)}, u32[]{:S(2)}) collective-permute-start(bf16[200,1024]{1,0:T(8,128)(2,1)S(1)} %collective-permute-done.10), channel_id=1, source_target_pairs={{0,56},{8,0},{16,8},{24,16},{32,24},{40,32},{48,40},{56,48},{1,57}... | collective-permute-start | bytes 1228808 | tf_op jit(solution)/shard_map/ppermute | solution.py:21
  38.8 2.2 %copy-start.11 = (bf16[200,1024]{1,0:T(8,128)(2,1)}, bf16[200,1024]{1,0:T(8,128)(2,1)S(1)}, u32[]{:S(2)}) copy-start(bf16[200,1024]{1,0:T(8,128)(2,1)S(1)} %collective-permute-done.9) | copy-start | bytes 1228804
  38.8 19.9 %collective-permute-start.11 = (bf16[200,1024]{1,0:T(8,128)(2,1)S(1)}, bf16[200,1024]{1,0:T(8,128)(2,1)S(1)}, u32[]{:S(2)}, u32[]{:S(2)}) collective-permute-start(bf16[200,1024]{1,0:T(8,128)(2,1)S(1)} %collective-permute-done.9), channel_id=1, source_target_pairs={{0,8},{8,16},{16,24},{24,32},{32,40},{40,48},{48,56},{56,0},{1,9},... | collective-permute-start | bytes 1228808 | tf_op jit(solution)/shard_map/ppermute | solution.py:21
  39.6 5.8 %copy-start.21 = (s32[32]{0:T(128)S(1)}, s32[32]{0:T(128)}, u32[]{:S(2)}) copy-start(s32[32]{0:T(128)} %param.18) | copy-start | bytes 388
  41.1 29.2 %all-to-all-start.1 = ((bf16[4,2,64,2,400]{4,2,3,1,0:T(8,128)(2,1)}), bf16[4,2,64,2,400]{4,2,3,1,0:T(8,128)(2,1)S(1)}, u32[]{:S(2)}, u32[]{:S(2)}) async-start(bf16[4,2,64,2,400]{4,2,3,1,0:T(8,128)(2,1)} %bitcast.9), calls=%async_computation.1 | async-start | bytes 2097152 | tf_op jit(solution)/shard_map/all_to_all | solution.py:29
  45.7 25.3 %copy-start.23 = (s32[32]{0:T(128)}, s32[32]{0:T(128)S(1)}, u32[]{:S(2)}) copy-start(s32[32]{0:T(128)S(1)} %reduce) | copy-start | bytes 388
  55.2 15.0 %copy-start.7 = (bf16[200,1024]{1,0:T(8,128)(2,1)}, bf16[200,1024]{1,0:T(8,128)(2,1)S(1)}, u32[]{:S(2)}) copy-start(bf16[200,1024]{1,0:T(8,128)(2,1)S(1)} %collective-permute-done.12) | copy-start | bytes 1228804
  55.2 10.1 %collective-permute-start.14 = (bf16[200,1024]{1,0:T(8,128)(2,1)S(1)}, bf16[200,1024]{1,0:T(8,128)(2,1)S(1)}, u32[]{:S(2)}, u32[]{:S(2)}) collective-permute-start(bf16[200,1024]{1,0:T(8,128)(2,1)S(1)} %collective-permute-done.12), channel_id=1, source_target_pairs={{0,56},{8,0},{16,8},{24,16},{32,24},{40,32},{48,40},{56,48},{1,57}... | collective-permute-start | bytes 1228808 | tf_op jit(solution)/shard_map/ppermute | solution.py:21
  58.7 12.3 %copy-start.13 = (bf16[200,1024]{1,0:T(8,128)(2,1)}, bf16[200,1024]{1,0:T(8,128)(2,1)S(1)}, u32[]{:S(2)}) copy-start(bf16[200,1024]{1,0:T(8,128)(2,1)S(1)} %collective-permute-done.11) | copy-start | bytes 1228804
  58.7 10.7 %collective-permute-start.13 = (bf16[200,1024]{1,0:T(8,128)(2,1)S(1)}, bf16[200,1024]{1,0:T(8,128)(2,1)S(1)}, u32[]{:S(2)}, u32[]{:S(2)}) collective-permute-start(bf16[200,1024]{1,0:T(8,128)(2,1)S(1)} %collective-permute-done.11), channel_id=1, source_target_pairs={{0,8},{8,16},{16,24},{24,32},{32,40},{40,48},{48,56},{56,0},{1,9},... | collective-permute-start | bytes 1228808 | tf_op jit(solution)/shard_map/ppermute | solution.py:21
  65.3 4.9 %copy-start.2 = (bf16[200,1024]{1,0:T(8,128)(2,1)}, bf16[200,1024]{1,0:T(8,128)(2,1)S(1)}, u32[]{:S(2)}) copy-start(bf16[200,1024]{1,0:T(8,128)(2,1)S(1)} %collective-permute-done.14) | copy-start | bytes 1228804
  66.0 15.5 %collective-permute-start.16 = (bf16[104,1024]{1,0:T(8,128)(2,1)}, bf16[104,1024]{1,0:T(8,128)(2,1)}, u32[]{:S(2)}, u32[]{:S(2)}) collective-permute-start(bf16[104,1024]{1,0:T(8,128)(2,1)} %slice.93), channel_id=1, source_target_pairs={{0,56},{8,0},{16,8},{24,16},{32,24},{40,32},{48,40},{56,48},{1,57}... | collective-permute-start | bytes 638984 | tf_op jit(solution)/shard_map/ppermute | solution.py:21
  69.4 0.9 copy-start.4
  70.2 11.4 %collective-permute-start.15 = (bf16[96,1024]{1,0:T(8,128)(2,1)}, bf16[96,1024]{1,0:T(8,128)(2,1)}, u32[]{:S(2)}, u32[]{:S(2)}) collective-permute-start(bf16[96,1024]{1,0:T(8,128)(2,1)} %slice.92), channel_id=1, source_target_pairs={{0,8},{8,16},{16,24},{24,32},{32,40},{40,48},{48,56},{56,0},{1,9},... | collective-permute-start | bytes 589832 | tf_op jit(solution)/shard_map/ppermute | solution.py:21
  72.1 1.0 copy-start.8
  72.8 1.0 copy-start.12
  73.1 1.0 copy-start.10
  73.9 1.0 copy-start.14
  74.9 1.0 copy-start.3
  75.9 7.0 %copy-start.5 = (bf16[200,1024]{1,0:T(8,128)(2,1)S(1)}, bf16[200,1024]{1,0:T(8,128)(2,1)}, u32[]{:S(2)}) copy-start(bf16[200,1024]{1,0:T(8,128)(2,1)} %copy-done.4) | copy-start | bytes 1228804
  82.9 14.8 %copy-start.17 = (pred[32]{0:T(512)(128)(4,1)S(1)}, pred[32]{0:T(512)(128)(4,1)}, u32[]{:S(2)}) copy-start(pred[32]{0:T(512)(128)(4,1)} %get-tuple-element.29) | copy-start | bytes 100
  82.9 14.8 %copy-start.18 = (pred[32]{0:T(512)(128)(4,1)S(1)}, pred[32]{0:T(512)(128)(4,1)}, u32[]{:S(2)}) copy-start(pred[32]{0:T(512)(128)(4,1)} %get-tuple-element.30) | copy-start | bytes 100
  82.9 14.8 %copy-start.19 = (pred[32]{0:T(512)(128)(4,1)S(1)}, pred[32]{0:T(512)(128)(4,1)}, u32[]{:S(2)}) copy-start(pred[32]{0:T(512)(128)(4,1)} %get-tuple-element.31) | copy-start | bytes 100
  82.9 14.8 %copy-start.20 = (pred[32]{0:T(512)(128)(4,1)S(1)}, pred[32]{0:T(512)(128)(4,1)}, u32[]{:S(2)}) copy-start(pred[32]{0:T(512)(128)(4,1)} %get-tuple-element.32) | copy-start | bytes 100
  83.3 19.6 %copy-start.22 = (s32[32]{0:T(128)S(1)}, s32[32]{0:T(128)}, u32[]{:S(2)}) copy-start(s32[32]{0:T(128)} %param.18) | copy-start | bytes 388
  83.3 19.6 %copy-start.24 = (s32[32]{0:T(128)S(1)}, s32[32]{0:T(128)}, u32[]{:S(2)}) copy-start(s32[32]{0:T(128)} %copy-done.23) | copy-start | bytes 388
  83.3 7.2 %collective-permute-start.17 = (bf16[64,1024]{1,0:T(8,128)(2,1)S(1)}, bf16[64,1024]{1,0:T(8,128)(2,1)S(1)}, u32[]{:S(2)}, u32[]{:S(2)}) collective-permute-start(bf16[64,1024]{1,0:T(8,128)(2,1)S(1)} %get-tuple-element.7), channel_id=1, source_target_pairs={{0,64},{64,0},{128,192},{192,128},{1,65},{65,1},{129,193},{193,129... | collective-permute-start | bytes 393224 | tf_op jit(solution)/shard_map/ppermute | solution.py:25
  83.9 13.7 %collective-permute-start.18 = (bf16[64,1024]{1,0:T(8,128)(2,1)S(1)}, bf16[64,1024]{1,0:T(8,128)(2,1)S(1)}, u32[]{:S(2)}, u32[]{:S(2)}) collective-permute-start(bf16[64,1024]{1,0:T(8,128)(2,1)S(1)} %get-tuple-element.9), channel_id=1, source_target_pairs={{0,128},{64,192},{128,0},{192,64},{1,129},{65,193},{129,1},{193,65... | collective-permute-start | bytes 393224 | tf_op jit(solution)/shard_map/ppermute | solution.py:25
  86.9 10.8 %collective-permute-start.19 = (bf16[64,1024]{1,0:T(8,128)(2,1)S(1)}, bf16[64,1024]{1,0:T(8,128)(2,1)S(1)}, u32[]{:S(2)}, u32[]{:S(2)}) collective-permute-start(bf16[64,1024]{1,0:T(8,128)(2,1)S(1)} %get-tuple-element.8), channel_id=1, source_target_pairs={{0,192},{64,128},{128,64},{192,0},{1,193},{65,129},{129,65},{193,1... | collective-permute-start | bytes 393224 | tf_op jit(solution)/shard_map/ppermute | solution.py:25
  99.0 22.3 %all-to-all-start.2 = ((bf16[32,8,1024]{2,1,0:T(8,128)(2,1)}), bf16[32,8,1024]{2,1,0:T(8,128)(2,1)S(1)}, u32[]{:S(2)}, u32[]{:S(2)}) async-start(bf16[32,8,1024]{2,1,0:T(8,128)(2,1)} %select_select_fusion), calls=%async_computation.2 | async-start | bytes 1048576 | tf_op jit(solution)/shard_map/all_to_all | solution.py:29
  102.9 24.3 %copy-start = (bf16[1,384,1024]{2,1,0:T(8,128)(2,1)S(1)}, bf16[1,384,1024]{2,1,0:T(8,128)(2,1)}, u32[]{:S(2)}) copy-start(bf16[1,384,1024]{2,1,0:T(8,128)(2,1)} %param.14) | copy-start | bytes 2359300
  122.9 15.1 %all-to-all-start.3 = ((bf16[4,128,1024]{2,1,0:T(8,128)(2,1)}), bf16[4,128,1024]{2,1,0:T(8,128)(2,1)}, u32[]{:S(2)}, u32[]{:S(2)}) async-start(bf16[4,128,1024]{2,1,0:T(8,128)(2,1)} %broadcast_in_dim.149), calls=%async_computation.3 | async-start | bytes 2097152 | tf_op jit(solution)/shard_map/all_to_all | solution.py:29
  127.2 27.0 %collective-permute-start.1 = (bf16[384,1024]{1,0:T(8,128)(2,1)S(1)}, bf16[384,1024]{1,0:T(8,128)(2,1)S(1)}, u32[]{:S(2)}, u32[]{:S(2)}) collective-permute-start(bf16[384,1024]{1,0:T(8,128)(2,1)S(1)} %bitcast.72), channel_id=1, source_target_pairs={{0,2},{2,4},{4,6},{6,0},{1,3},{3,5},{5,7},{7,1},{8,10},{10,12},{12... | collective-permute-start | bytes 2359304 | tf_op jit(solution)/shard_map/ppermute | solution.py:21
  128.6 26.3 %collective-permute-start.3 = (bf16[384,1024]{1,0:T(8,128)(2,1)S(1)}, bf16[384,1024]{1,0:T(8,128)(2,1)S(1)}, u32[]{:S(2)}, u32[]{:S(2)}) collective-permute-start(bf16[384,1024]{1,0:T(8,128)(2,1)S(1)} %bitcast.73), channel_id=1, source_target_pairs={{0,6},{2,0},{4,2},{6,4},{1,7},{3,1},{5,3},{7,5},{8,14},{10,8},{12,... | collective-permute-start | bytes 2359304 | tf_op jit(solution)/shard_map/ppermute | solution.py:21
  130.0 35.0 %collective-permute-start = (bf16[384,1024]{1,0:T(8,128)(2,1)S(1)}, bf16[384,1024]{1,0:T(8,128)(2,1)S(1)}, u32[]{:S(2)}, u32[]{:S(2)}) collective-permute-start(bf16[384,1024]{1,0:T(8,128)(2,1)S(1)} %bitcast.74), channel_id=1, source_target_pairs={{0,1},{1,0},{2,3},{3,2},{4,5},{5,4},{6,7},{7,6},{8,9},{9,8},{10,11... | collective-permute-start | bytes 2359304 | tf_op jit(solution)/shard_map/ppermute | solution.py:21
  138.1 35.7 %collective-permute-start.20 = (bf16[4,128,1024]{2,1,0:T(8,128)(2,1)}, bf16[4,128,1024]{2,1,0:T(8,128)(2,1)}, u32[]{:S(2)}, u32[]{:S(2)}) collective-permute-start(bf16[4,128,1024]{2,1,0:T(8,128)(2,1)} %all-to-all-done.3.refs_10_), channel_id=1, source_target_pairs={{0,1},{1,0},{2,3},{3,2},{4,5},{5,4},{6,7},{7,6},{8,9},{9,8},{10,11... | collective-permute-start | bytes 3145736 | tf_op jit(solution)/shard_map/ppermute | solution.py:21
  155.0 11.3 %collective-permute-start.5 = (bf16[192,1024]{1,0:T(8,128)(2,1)}, bf16[192,1024]{1,0:T(8,128)(2,1)S(1)}, u32[]{:S(2)}, u32[]{:S(2)}) collective-permute-start(bf16[192,1024]{1,0:T(8,128)(2,1)} %slice.90), channel_id=1, source_target_pairs={{0,2},{2,4},{4,6},{6,0},{1,3},{3,5},{5,7},{7,1},{8,10},{10,12},{12... | collective-permute-start | bytes 1179656 | tf_op jit(solution)/shard_map/ppermute | solution.py:21
  155.8 14.4 %collective-permute-start.7 = (bf16[192,1024]{1,0:T(8,128)(2,1)}, bf16[192,1024]{1,0:T(8,128)(2,1)}, u32[]{:S(2)}, u32[]{:S(2)}) collective-permute-start(bf16[192,1024]{1,0:T(8,128)(2,1)} %slice.91), channel_id=1, source_target_pairs={{0,6},{2,0},{4,2},{6,4},{1,7},{3,1},{5,3},{7,5},{8,14},{10,8},{12,... | collective-permute-start | bytes 1179656 | tf_op jit(solution)/shard_map/ppermute | solution.py:21
  158.4 15.4 %collective-permute-start.2 = (bf16[384,1024]{1,0:T(8,128)(2,1)S(1)}, bf16[384,1024]{1,0:T(8,128)(2,1)}, u32[]{:S(2)}, u32[]{:S(2)}) collective-permute-start(bf16[384,1024]{1,0:T(8,128)(2,1)S(1)} %collective-permute-done.1.refs_2_), channel_id=1, source_target_pairs={{0,1},{1,0},{2,3},{3,2},{4,5},{5,4},{6,7},{7,6},{8,9},{9,8},{10,11... | collective-permute-start | bytes 2359304 | tf_op jit(solution)/shard_map/ppermute | solution.py:21
  165.0 8.8 %collective-permute-start.4 = (bf16[384,1024]{1,0:T(8,128)(2,1)S(1)}, bf16[384,1024]{1,0:T(8,128)(2,1)}, u32[]{:S(2)}, u32[]{:S(2)}) collective-permute-start(bf16[384,1024]{1,0:T(8,128)(2,1)S(1)} %collective-permute-done.3.refs_4_), channel_id=1, source_target_pairs={{0,1},{1,0},{2,3},{3,2},{4,5},{5,4},{6,7},{7,6},{8,9},{9,8},{10,11... | collective-permute-start | bytes 2359304 | tf_op jit(solution)/shard_map/ppermute | solution.py:21
  166.3 7.5 %collective-permute-start.6 = (bf16[192,1024]{1,0:T(8,128)(2,1)S(1)}, bf16[192,1024]{1,0:T(8,128)(2,1)}, u32[]{:S(2)}, u32[]{:S(2)}) collective-permute-start(bf16[192,1024]{1,0:T(8,128)(2,1)S(1)} %collective-permute-done.5.refs_6_), channel_id=1, source_target_pairs={{0,1},{1,0},{2,3},{3,2},{4,5},{5,4},{6,7},{7,6},{8,9},{9,8},{10,11... | collective-permute-start | bytes 1179656 | tf_op jit(solution)/shard_map/ppermute | solution.py:21
  170.1 3.6 %collective-permute-start.8 = (bf16[192,1024]{1,0:T(8,128)(2,1)}, bf16[192,1024]{1,0:T(8,128)(2,1)}, u32[]{:S(2)}, u32[]{:S(2)}) collective-permute-start(bf16[192,1024]{1,0:T(8,128)(2,1)} %collective-permute-done.7.refs_8_), channel_id=1, source_target_pairs={{0,1},{1,0},{2,3},{3,2},{4,5},{5,4},{6,7},{7,6},{8,9},{9,8},{10,11... | collective-permute-start | bytes 1179656 | tf_op jit(solution)/shard_map/ppermute | solution.py:21
  173.8 0.8 copy-start.1
Sparse Core Ops, SparseCore 0:
  9.9 137.3 all-gather.1
